TPU v7x, 32 devices: a whole 2x2x4 slice. The times are simulated.
32 devices in a mesh: layer: 4 (over y, x), row: 2 (over core), col: 4 (over z).
Axes of the slice: x: 2, y: 2, z: 4, core: 2. Of those that a mesh axis runs over, the one named last changes fastest.
Arguments:
- block_values: bfloat16 [4, 2, 4, 32, 256, 256], P('layer', 'row', 'col'), may hold values from 0 to 3
- block_rows: int32 [4, 2, 4, 32], P('layer', 'row', 'col'), may hold values from 0 to 255
- block_cols: int32 [4, 2, 4, 32], P('layer', 'row', 'col'), may hold values from 0 to 127
- block_count: int32 [4, 2, 4], P('layer', 'row', 'col'), may hold values from 1 to 32, as said below
- dangling: int32 [4, 2, 4, 16384], P('layer', 'row', 'col'), may hold values 0 or 1
- start_ranks: float32 [4, 2, 4, 16384], P('layer', 'row', 'col'), may hold values from 0.2 to 5
Outputs:
- ranks: float32 [4, 2, 4, 16384], P('layer', 'row', 'col')
- residuals: float32 [3, 4], P(None, 'layer')
Inputs may be any that keep to these rules, and one draw needn't show every extreme that they name: `block_count`: live slots of a tile; in every layer some tile has all 32 slots live. `block_rows`: slots at or past a tile's count carry no edges; coordinates may repeat within a tile, and repeated blocks add.
All inputs are finite; a program needn't handle non-finite values. No bound on the sum of `dangling` on one device may be relied on, other than what follows from the above.
Results may differ from a plain program's by a relative error of at most 0.0012.
Values may be sent and summed in bfloat16 or wider, within the bound.
A program may use at most 64 MiB of HBM per device.

v0:
```python
import functools

import jax
import jax.numpy as jnp
from jax import lax
from jax.experimental import pallas as pl
from jax.experimental.pallas import tpu as pltpu
from jax.sharding import PartitionSpec as P

ITERS = 3
CHUNK = 16

damping = 0.85
coupling = 0.3


def fold(v):
    rows, lanes = v.shape
    acc = v[:, 0:128]
    for h in range(1, lanes // 128):
        acc = acc + v[:, h * 128 : (h + 1) * 128]
    return jnp.sum(acc.reshape(rows // 8, 8, 128), axis=0)


def split(v):
    hi = v.astype(jnp.bfloat16)
    lo = (v - hi.astype(jnp.float32)).astype(jnp.bfloat16)
    return hi, lo


def dot(a, b):
    return jnp.dot(a, b, preferred_element_type=jnp.float32)


def kernel(
    nl, nr, nc, nodes,
    values_hbm, rows_ref, cols_ref, count_ref, dang_hbm, start_hbm,
    ranks_ref, resid_ref,
    values, dang_in, start_in, x_ref, inv_ref, kinv_ref,
    colsum, ohrow, ohcol, own_prod, chg,
    px_recv, pd_recv, col_send, col_recv, cs_recv, row_send, row_recv,
    sc_send, sc_recv, ma_send, ma_recv,
    pr_send, pr_recv, sp_send, sp_recv, rs_send, rs_recv,
    sem_in, sem_v,
    px_ss, px_rs, pd_ss, pd_rs, col_ss, col_rs, cs_ss, cs_rs, row_ss, row_rs, sc_ss, sc_rs, ma_ss, ma_rs,
    pr_ss, pr_rs, sp_ss, sp_rs, rs_ss, rs_rs,
):
    l, r, c = (lax.axis_index(a) for a in ("layer", "row", "col"))
    slots, edge, _ = values.shape
    blocks = x_ref.shape[0]
    halves = edge // 128
    nchunk = slots // CHUNK
    f32, bf16 = jnp.float32, jnp.bfloat16

    def remote(src, dst, ss, rs, ll, rr, cc):
        return pltpu.make_async_remote_copy(
            src_ref=src, dst_ref=dst, send_sem=ss, recv_sem=rs,
            device_id=(ll, rr, cc), device_id_type=pl.DeviceIdType.MESH,
        )

    in_d = pltpu.make_async_copy(dang_hbm, dang_in, sem_in.at[0])
    in_x = pltpu.make_async_copy(start_hbm, start_in, sem_in.at[1])
    vcopies = [
        pltpu.make_async_copy(
            values_hbm.at[pl.ds(k * CHUNK, CHUNK)], values.at[pl.ds(k * CHUNK, CHUNK)], sem_v.at[k]
        )
        for k in range(nchunk)
    ]
    in_x.start()
    in_d.start()
    for cp in vcopies:
        cp.start()

    peers = [(dr, dc) for dr in range(nr) for dc in range(nc) if (dr, dc) != (0, 0)]
    barrier = pltpu.get_barrier_semaphore()
    for dr, dc in peers:
        pl.semaphore_signal(
            barrier, inc=1,
            device_id=(l, lax.rem(r + dr, nr), lax.rem(c + dc, nc)),
            device_id_type=pl.DeviceIdType.MESH,
        )

    @pl.when(l > 0)
    def _():
        pl.semaphore_signal(
            barrier, inc=1, device_id=(l - 1, r, c), device_id_type=pl.DeviceIdType.MESH)

    @pl.when(l < nl - 1)
    def _():
        pl.semaphore_signal(
            barrier, inc=1, device_id=(l + 1, r, c), device_id_type=pl.DeviceIdType.MESH)

    live = lax.broadcasted_iota(jnp.int32, (1, slots), 1) < count_ref[...]
    rows = jnp.where(live, rows_ref[...], -1)
    cols = jnp.where(live, cols_ref[...], -1)
    row_send[...] = jnp.broadcast_to(
        jnp.concatenate([rows, jnp.full((1, 128 - slots), -1, jnp.int32)], axis=1), (8, 128)
    ).astype(f32)
    col_send[...] = jnp.broadcast_to(
        jnp.concatenate([cols, jnp.full((1, 128 - slots), -1, jnp.int32)], axis=1), (8, 128)
    ).astype(f32)

    eye = lax.broadcasted_iota(jnp.int32, (slots, slots), 0) == lax.broadcasted_iota(
        jnp.int32, (slots, slots), 1)
    colv = jnp.sum(
        jnp.where(eye, jnp.broadcast_to(cols_ref[...], (slots, slots)).astype(f32), 0.0),
        axis=1, keepdims=True,
    )
    for d in range(nr):
        base = lax.rem(r - d + nr, nr) * blocks
        at = (lax.broadcasted_iota(jnp.int32, (slots, blocks), 1) + base).astype(f32)
        ohcol[d] = jnp.where(colv == at, 1.0, 0.0).astype(bf16)

    ones = jnp.ones((CHUNK, edge), bf16)
    rid = lax.broadcasted_iota(jnp.int32, (CHUNK, edge), 0)

    def column_sum(k):
        vcopies[k].wait()
        acc = jnp.zeros((CHUNK, edge), f32)
        for s in range(CHUNK):
            acc = jnp.where(rid == s, dot(ones, values[k * CHUNK + s]), acc)
        colsum[k] = acc

    in_x.wait()
    in_d.wait()
    for h in range(halves):
        x_ref[:, h * 128 : (h + 1) * 128] = start_in[pl.ds(h, blocks, stride=halves), :]
    column_sum(0)

    order = []
    first, last = jnp.int32(0), jnp.int32(nc - 1)
    for _ in range(nc - 1):
        left = (c - first >= last - c).astype(jnp.int32)
        order.append(left * first + (1 - left) * last)
        first, last = first + left, last - (1 - left)
    far = [(cc, lax.rem(cc - c + nc, nc)) for cc in order]
    far_peers = [(dr, cc, d) for cc, d in far for dr in range(nr)]
    far_peers += [(dr, c, 0) for dr in range(1, nr)]
    sent = []

    pl.semaphore_wait(
        barrier, len(peers) + (l > 0).astype(jnp.int32) + (l < nl - 1).astype(jnp.int32))

    px, pd, pc, pcs, prow = [], [], [], [], []
    for d in range(1, nr):
        rr = lax.rem(r + d, nr)
        px.append(remote(start_in, px_recv.at[d], px_ss.at[d], px_rs.at[d], l, rr, c))
        pd.append(remote(dang_in, pd_recv.at[d], pd_ss.at[d], pd_rs.at[d], l, rr, c))
        pc.append(remote(col_send, col_recv.at[d], col_ss.at[d], col_rs.at[d], l, rr, c))
        pcs.append([
            remote(colsum.at[k], cs_recv.at[d, k], cs_ss.at[d, k], cs_rs.at[d, k], l, rr, c)
            for k in range(nchunk)
        ])
    for cc, d in far:
        prow.append(remote(row_send, row_recv.at[d], row_ss.at[d], row_rs.at[d], l, r, cc))
    for cp in px + pd + pc + prow + [q[0] for q in pcs]:
        cp.start()

    def spill_copies(t):
        return (
            remote(sp_send.at[t], sp_recv.at[t, 0], sp_ss.at[t, 0], sp_rs.at[t, 0], l + 1, r, c),
            remote(sp_send.at[t], sp_recv.at[t, 1], sp_ss.at[t, 1], sp_rs.at[t, 1], l - 1, r, c),
        )

    spread = jnp.where((l == 0) | (l == nl - 1), 1.0, 0.5).astype(f32) * coupling

    def send_spill(t, x):
        sp_send[t] = (x * spread).astype(sp_send.dtype)
        up, down = spill_copies(t)

        @pl.when(l < nl - 1)
        def _():
            up.start()

        @pl.when(l > 0)
        def _():
            down.start()

    @pl.when(l == 0)
    def _():
        for t in range(ITERS):
            sp_recv[t, 0] = jnp.zeros((blocks, edge), sp_recv.dtype)

    @pl.when(l == nl - 1)
    def _():
        for t in range(ITERS):
            sp_recv[t, 1] = jnp.zeros((blocks, edge), sp_recv.dtype)

    send_spill(0, x_ref[...])

    for k in range(1, nchunk):
        column_sum(k)
        for q in pcs:
            q[k].start()

    def spread_sums(tab, sums, rr):
        at = (lax.broadcasted_iota(jnp.int32, (blocks, slots), 0) + rr * blocks).astype(f32)
        oh = jnp.where(
            jnp.broadcast_to(tab[0:1, 0:slots], (blocks, slots)) == at, 1.0, 0.0).astype(bf16)
        hi, lo = split(sums.reshape(slots, edge))
        return dot(oh, hi) + dot(oh, lo)

    def piece(buf, h):
        return buf[pl.ds(h, blocks, stride=halves), :]

    near = [spread_sums(col_send, colsum[...], lax.rem(r - d + nr, nr)) for d in range(nr)]
    for cp in px + pd + pc:
        cp.wait_recv()
    peer_x = {d: jnp.concatenate([piece(px_recv.at[d], h) for h in range(halves)], axis=1)
              for d in range(1, nr)}
    keeps = {d: 1.0 - jnp.concatenate(
        [piece(pd_recv.at[d] if d else dang_in, h) for h in range(halves)], axis=1).astype(f32)
        for d in range(nr)}
    for q in pcs:
        for cp in q:
            cp.wait_recv()
    for d in range(nr):
        deg = near[d]
        for e in range(1, nr):
            deg = deg + spread_sums(col_recv[e], cs_recv[e], lax.rem(r - d + nr, nr))
        inv = 1.0 / (keeps[d] * deg + 1.0)
        kinv = keeps[d] * inv
        if d == 0:
            inv_ref[...] = inv
            kinv_ref[...] = kinv
        else:
            sc_recv[0, d] = (peer_x[d] * kinv).astype(bf16)

    def row_onehot(tab):
        at = (lax.broadcasted_iota(jnp.int32, (blocks, slots), 0) + c * blocks).astype(f32)
        return jnp.where(jnp.broadcast_to(tab[0:1, 0:slots], (blocks, slots)) == at,
                         1.0, 0.0).astype(bf16)

    def step(t):
        x = x_ref[...]
        scaled = (x * kinv_ref[...]).astype(bf16)
        if t > 0:
            sc_send[t] = scaled
        sc = [
            remote(sc_send.at[t], sc_recv.at[t, d], sc_ss.at[t, d], sc_rs.at[t, d],
                   l, lax.rem(r + d, nr), c)
            for d in range(1, nr)
            if t > 0
        ]
        for cp in sc:
            cp.start()
        mass_own = jnp.sum(fold(x * inv_ref[...]), axis=0, keepdims=True)
        ma_send[t] = mass_own
        ma = []
        for i, (dr, cc, dc) in enumerate(far_peers):
            slot = dr * nc + dc - 1
            ma.append(remote(ma_send.at[t], ma_recv.at[t, slot], ma_ss.at[t, slot],
                             ma_rs.at[t, slot], l, lax.rem(r + dr, nr), cc))
        for cp in ma:
            cp.start()

        if t > 0:
            send_spill(t, x)

        picked = dot(ohcol[0], scaled)
        for d in range(1, nr):
            if t > 0:
                sc[d - 1].wait_recv()
            picked = picked + dot(ohcol[d], sc_recv[t, d])
        picked = picked.astype(bf16)

        pr = []
        for k in range(nchunk):
            lhs = picked[k * CHUNK : (k + 1) * CHUNK]
            acc = jnp.zeros((CHUNK, edge), f32)
            for s in range(CHUNK):
                res = lax.dot_general(
                    lhs, values[k * CHUNK + s], (((1,), (1,)), ((), ())),
                    preferred_element_type=f32)
                acc = jnp.where(rid == s, res, acc)
            own_prod[k * CHUNK : (k + 1) * CHUNK] = acc
            pr_send[t, k] = acc.astype(pr_send.dtype)
            for cc, d in far:
                cp = remote(pr_send.at[t, k], pr_recv.at[t, d, k], pr_ss.at[t, d, k],
                            pr_rs.at[t, d, k], l, r, cc)
                cp.start()
                pr.append(cp)

        if t == 0:
            ohrow[0] = row_onehot(row_send)
            for cp in prow:
                cp.wait_recv()
            for d in range(1, nc):
                ohrow[d] = row_onehot(row_recv[d])

        phi, plo = split(own_prod[...])
        walk = dot(ohrow[0], phi) + dot(ohrow[0], plo)

        up, down = spill_copies(t)

        @pl.when(l > 0)
        def _():
            up.wait_recv()

        @pl.when(l < nl - 1)
        def _():
            down.wait_recv()

        arrive = sp_recv[t, 0].astype(f32) + sp_recv[t, 1].astype(f32)
        mass = mass_own
        for cp in ma:
            cp.wait_recv()
        for i in range(len(peers)):
            mass = mass + ma_recv[t, i]
        rest = damping * ((1.0 - coupling) * (jnp.sum(mass) / nodes) + arrive) + (1.0 - damping)

        for d in range(1, nc):
            for k in range(nchunk):
                remote(pr_send.at[t, k], pr_recv.at[t, d, k], pr_ss.at[t, d, k], pr_rs.at[t, d, k], l, r, lax.rem(c + d, nc)).wait_recv()
            got = pr_recv[t, d].reshape(slots, edge)
            if got.dtype == bf16:
                walk = walk + dot(ohrow[d], got)
            else:
                ghi, glo = split(got)
                walk = walk + dot(ohrow[d], ghi) + dot(ohrow[d], glo)
        updated = damping * (1.0 - coupling) * walk + rest
        x_ref[...] = updated
        chg[t] = fold(jnp.abs(updated - x))

        sent.extend(sc + ma + pr)

    for t in range(ITERS):
        step(t)

    lane = lax.broadcasted_iota(jnp.int32, (1, 128), 1)
    changes = jnp.zeros((1, 128), f32)
    for t in range(ITERS):
        changes = jnp.where(lane == t, jnp.sum(chg[t]), changes)
    rs_send[...] = changes
    rs = []
    for dr, cc, dc in far_peers:
        i = dr * nc + dc - 1
        cp = remote(rs_send, rs_recv.at[i], rs_ss.at[i], rs_rs.at[i],
                    l, lax.rem(r + dr, nr), cc)
        cp.start()
        rs.append(cp)
    for h in range(halves):
        ranks_ref[pl.ds(h, blocks, stride=halves), :] = x_ref[:, h * 128 : (h + 1) * 128]
    for cp in px + pd + pc + prow + [e for q in pcs for e in q] + sent:
        cp.wait_send()
    ups = [spill_copies(t) for t in range(ITERS)]

    @pl.when(l < nl - 1)
    def _():
        for up, _ in ups:
            up.wait_send()

    @pl.when(l > 0)
    def _():
        for _, down in ups:
            down.wait_send()

    total = rs_send[...]
    for cp in rs:
        cp.wait_recv()
    for i in range(len(peers)):
        total = total + rs_recv[i]
    resid_ref[...] = total
    for cp in rs:
        cp.wait_send()


def finish(ranks_in, resid_in, ranks_ref, resid_ref):
    ranks_ref[...] = ranks_in[...]
    resid_ref[...] = resid_in[:, 0:ITERS]


def local(block_values, block_rows, block_cols, block_count, dangling, start_ranks):
    span = start_ranks.shape[-1]
    nl, nr, nc = (lax.axis_size(a) for a in ("layer", "row", "col"))
    slots, edge = block_values.shape[3], block_values.shape[-1]
    blocks = span // edge
    nchunk = slots // CHUNK
    nodes = nr * nc * span
    npeer = nr * nc - 1
    f32, bf16 = jnp.float32, jnp.bfloat16
    vm, dma = pltpu.VMEM, pltpu.SemaphoreType.DMA
    big = (blocks, edge)
    PT, ST = bf16, f32
    scratch = [
        vm((slots, edge, edge), bf16), vm((span // 128, 128), jnp.int32), vm((span // 128, 128), f32),
        vm(big, f32), vm(big, f32), vm(big, f32),
        vm((nchunk, CHUNK, edge), f32), vm((nc, blocks, slots), bf16), vm((nr, slots, blocks), bf16),
        vm((slots, edge), f32), vm((ITERS, 8, 128), f32),
        vm((nr, span // 128, 128), f32), vm((nr, span // 128, 128), jnp.int32),
        vm((8, 128), f32), vm((nr, 8, 128), f32), vm((nr, nchunk, CHUNK, edge), f32),
        vm((8, 128), f32), vm((nc, 8, 128), f32),
        vm((ITERS,) + big, bf16), vm((ITERS, nr) + big, bf16),
        vm((ITERS, 1, 128), f32), vm((ITERS, npeer, 1, 128), f32),
        vm((ITERS, nchunk, CHUNK, edge), PT), vm((ITERS, nc, nchunk, CHUNK, edge), PT),
        vm((ITERS,) + big, ST), vm((ITERS, 2) + big, ST),
        vm((1, 128), f32), vm((npeer, 1, 128), f32),
        dma((2,)), dma((nchunk,)),
        dma((nr,)), dma((nr,)), dma((nr,)), dma((nr,)), dma((nr,)), dma((nr,)),
        dma((nr, nchunk)), dma((nr, nchunk)), dma((nc,)), dma((nc,)),
        dma((ITERS, nr)), dma((ITERS, nr)), dma((ITERS, npeer)), dma((ITERS, npeer)),
        dma((ITERS, nc, nchunk)), dma((ITERS, nc, nchunk)),
        dma((ITERS, 2)), dma((ITERS, 2)), dma((npeer,)), dma((npeer,)),
    ]
    hbm = pl.BlockSpec(memory_space=pltpu.HBM)
    vmem = pl.BlockSpec(memory_space=pltpu.VMEM)
    ranks, resid = pl.pallas_call(
        functools.partial(kernel, nl, nr, nc, nodes),
        out_shape=(
            pltpu.VMEM((span // 128, 128), f32),
            pltpu.VMEM((1, 128), f32),
        ),
        in_specs=[hbm, vmem, vmem, vmem, hbm, hbm],
        out_specs=(vmem, vmem),
        scratch_shapes=scratch,
        compiler_params=pltpu.CompilerParams(collective_id=0, has_side_effects=True),
    )(
        block_values.reshape(slots, edge, edge),
        block_rows.reshape(1, slots),
        block_cols.reshape(1, slots),
        block_count.reshape(1, 1),
        dangling.reshape(span // 128, 128),
        start_ranks.reshape(span // 128, 128),
    )
    ranks, resid = pl.pallas_call(
        finish,
        out_shape=(
            jax.ShapeDtypeStruct((span // 128, 128), f32),
            jax.ShapeDtypeStruct((1, ITERS), f32),
        ),
        in_specs=[vmem, vmem],
        out_specs=(vmem, vmem),
        compiler_params=pltpu.CompilerParams(vmem_limit_bytes=4 * 1024 * 1024),
    )(ranks, resid)
    return ranks.reshape(1, 1, 1, span), resid.T


def solution(mesh):
    placed = (
        P("layer", "row", "col", None, None, None),
        P("layer", "row", "col", None),
        P("layer", "row", "col", None),
        P("layer", "row", "col"),
        P("layer", "row", "col", None),
        P("layer", "row", "col", None),
    )
    return jax.shard_map(
        local,
        mesh=mesh,
        in_specs=placed,
        out_specs=(P("layer", "row", "col", None), P(None, "layer")),
        check_vma=False,
    )
```

profile of v0, /device:TPU:0, one launch (start us, length us, event | category | flops | bytes accessed | tf_op | source)
XLA Modules:
  0.0 30.4 jit_solution(6775174844861136523)
XLA Ops:
  1.3 28.5 %shard_map.77 = (f32[128,128]{1,0:T(8,128)S(1)}, f32[1,128]{1,0:T(1,128)S(1)}) custom-call(bf16[32,256,256]{2,1,0:T(8,128)(2,1)} %bitcast.9, s32[1,32]{1,0:T(1,128)} %bitcast.12, s32[1,32]{1,0:T(1,128)} %bitcast.13, s32[1,1]{1,0:T(1,128)} %bitcast.8.count_ref, s32[128,128]{1,0:T(8,128)} %bitcast.10, f32[128,128]{1,0:T(8,128)} %bitcast.11), custom_call_target="tpu_custom_call" | custom-call | tf_op jit(solution)/shard_map/pallas_call | solution.py:407
  29.8 0.6 %shard_map.78 = (f32[128,128]{1,0:T(8,128)}, f32[1,3]{1,0:T(1,128)}) custom-call(f32[128,128]{1,0:T(8,128)S(1)} %get-tuple-element.6.ranks_in, f32[1,128]{1,0:T(1,128)S(1)} %get-tuple-element.7.resid_in), custom_call_target="tpu_custom_call" | custom-call | tf_op jit(solution)/shard_map/pallas_call | solution.py:425
where the time goes:
time: 30.6 us; the launch traced here: 30.4 us
  Pallas kernels  29.1 us (95%)
  between operations  1.28 us (4%)
    pallas_call x1, Pallas kernels, local(): pl.pallas_call(functools.partial(kernel, nl, nr, nc, nodes), out_shape=(p...  28.5 us
    pallas_call x1, Pallas kernels, local(): pl.pallas_call(finish, out_shape=(jax.ShapeDtypeStruct((span // 128, 128)...  0.64 us

commit v1 on v0

--- a/solution.py
+++ b/solution.py
@@ -34,13 +34,14 @@
 
 def kernel(
     nl, nr, nc, nodes,
-    values_hbm, rows_ref, cols_ref, count_ref, dang_hbm, start_hbm,
+    values_hbm, rows_hbm, cols_hbm, count_hbm, dang_hbm, start_hbm,
     ranks_ref, resid_ref,
     values, dang_in, start_in, x_ref, inv_ref, kinv_ref,
     colsum, ohrow, ohcol, own_prod, chg,
     px_recv, pd_recv, col_send, col_recv, cs_recv, row_send, row_recv,
     sc_send, sc_recv, ma_send, ma_recv,
     pr_send, pr_recv, sp_send, sp_recv, rs_send, rs_recv,
+    rows_ref, cols_ref, count_ref,
     sem_in, sem_v,
     px_ss, px_rs, pd_ss, pd_rs, col_ss, col_rs, cs_ss, cs_rs, row_ss, row_rs, sc_ss, sc_rs, ma_ss, ma_rs,
     pr_ss, pr_rs, sp_ss, sp_rs, rs_ss, rs_rs,
@@ -66,10 +67,17 @@
         )
         for k in range(nchunk)
     ]
+    small = [
+        pltpu.make_async_copy(src, dst, sem_in.at[2 + i])
+        for i, (src, dst) in enumerate(
+            [(rows_hbm, rows_ref), (cols_hbm, cols_ref), (count_hbm, count_ref)])
+    ]
     in_x.start()
     in_d.start()
+    for cp in small:
+        cp.start()
     for cp in vcopies:
-        cp.start()
+        cp.start(priority=1)
 
     peers = [(dr, dc) for dr in range(nr) for dc in range(nc) if (dr, dc) != (0, 0)]
     barrier = pltpu.get_barrier_semaphore()
@@ -90,6 +98,8 @@
         pl.semaphore_signal(
             barrier, inc=1, device_id=(l + 1, r, c), device_id_type=pl.DeviceIdType.MESH)
 
+    for cp in small:
+        cp.wait()
     live = lax.broadcasted_iota(jnp.int32, (1, slots), 1) < count_ref[...]
     rows = jnp.where(live, rows_ref[...], -1)
     cols = jnp.where(live, cols_ref[...], -1)
@@ -365,6 +375,10 @@
         cp.wait_send()
 
 
+def scoped(sems, *args):
+    pl.run_scoped(lambda *refs: kernel(*args, *refs), *sems)
+
+
 def finish(ranks_in, resid_in, ranks_ref, resid_ref):
     ranks_ref[...] = ranks_in[...]
     resid_ref[...] = resid_in[:, 0:ITERS]
@@ -381,7 +395,7 @@
     f32, bf16 = jnp.float32, jnp.bfloat16
     vm, dma = pltpu.VMEM, pltpu.SemaphoreType.DMA
     big = (blocks, edge)
-    PT, ST = bf16, f32
+    PT, ST = bf16, bf16
     scratch = [
         vm((slots, edge, edge), bf16), vm((span // 128, 128), jnp.int32), vm((span // 128, 128), f32),
         vm(big, f32), vm(big, f32), vm(big, f32),
@@ -395,7 +409,10 @@
         vm((ITERS, nchunk, CHUNK, edge), PT), vm((ITERS, nc, nchunk, CHUNK, edge), PT),
         vm((ITERS,) + big, ST), vm((ITERS, 2) + big, ST),
         vm((1, 128), f32), vm((npeer, 1, 128), f32),
-        dma((2,)), dma((nchunk,)),
+        vm((1, slots), jnp.int32), vm((1, slots), jnp.int32), vm((1, 1), jnp.int32),
+    ]
+    sems = [
+        dma((5,)), dma((nchunk,)),
         dma((nr,)), dma((nr,)), dma((nr,)), dma((nr,)), dma((nr,)), dma((nr,)),
         dma((nr, nchunk)), dma((nr, nchunk)), dma((nc,)), dma((nc,)),
         dma((ITERS, nr)), dma((ITERS, nr)), dma((ITERS, npeer)), dma((ITERS, npeer)),
@@ -405,12 +422,12 @@
     hbm = pl.BlockSpec(memory_space=pltpu.HBM)
     vmem = pl.BlockSpec(memory_space=pltpu.VMEM)
     ranks, resid = pl.pallas_call(
-        functools.partial(kernel, nl, nr, nc, nodes),
+        functools.partial(scoped, sems, nl, nr, nc, nodes),
         out_shape=(
             pltpu.VMEM((span // 128, 128), f32),
             pltpu.VMEM((1, 128), f32),
         ),
-        in_specs=[hbm, vmem, vmem, vmem, hbm, hbm],
+        in_specs=[hbm] * 6,
         out_specs=(vmem, vmem),
         scratch_shapes=scratch,
         compiler_params=pltpu.CompilerParams(collective_id=0, has_side_effects=True),

time: 30.6 us -> 28.5 us (0.931)
  Pallas kernels: 29.1 us -> 27.1 us
    pallas_call x1, Pallas kernels: 28.5 us -> 26.5 us  [local(): pl.pallas_call(functools.partial(scoped, sems, nl, nr, nc, nodes), out_sh...]
where the time goes in v1:
time: 28.5 us; the launch traced here: 28.4 us
  Pallas kernels  27.1 us (95%)
  between operations  1.28 us (4%)
    pallas_call x1, Pallas kernels, local(): pl.pallas_call(functools.partial(scoped, sems, nl, nr, nc, nodes), out_sh...  26.5 us
    pallas_call x1, Pallas kernels, local(): pl.pallas_call(finish, out_shape=(jax.ShapeDtypeStruct((span // 128, 128)...  0.64 us

profile of v1, /device:TPU:0, one launch (start us, length us, event | category | flops | bytes accessed | tf_op | source)
XLA Modules:
  0.0 28.4 jit_solution(1005268580771882867)
XLA Ops:
  1.3 26.5 %shard_map.77 = (f32[128,128]{1,0:T(8,128)S(1)}, f32[1,128]{1,0:T(1,128)S(1)}) custom-call(bf16[32,256,256]{2,1,0:T(8,128)(2,1)} %bitcast.9, s32[1,32]{1,0:T(1,128)} %bitcast.12, s32[1,32]{1,0:T(1,128)} %bitcast.13, s32[1,1]{1,0:T(1,128)} %bitcast.8.args_3_, s32[128,128]{1,0:T(8,128)} %bitcast.10, f32[128,128]{1,0:T(8,128)} %bitcast.11), custom_call_target="tpu_custom_call" | custom-call | tf_op jit(solution)/shard_map/pallas_call | solution.py:424
  27.7 0.6 %shard_map.78 = (f32[128,128]{1,0:T(8,128)}, f32[1,3]{1,0:T(1,128)}) custom-call(f32[128,128]{1,0:T(8,128)S(1)} %get-tuple-element.6.ranks_in, f32[1,128]{1,0:T(1,128)S(1)} %get-tuple-element.7.resid_in), custom_call_target="tpu_custom_call" | custom-call | tf_op jit(solution)/shard_map/pallas_call | solution.py:442

commit v2 on v1

--- a/solution.py
+++ b/solution.py
@@ -9,6 +9,8 @@
 
 ITERS = 3
 CHUNK = 16
+PIECE = 8
+CUTS = (16, 16)
 
 damping = 0.85
 coupling = 0.3
@@ -36,10 +38,11 @@
     nl, nr, nc, nodes,
     values_hbm, rows_hbm, cols_hbm, count_hbm, dang_hbm, start_hbm,
     ranks_ref, resid_ref,
-    values, dang_in, start_in, x_ref, inv_ref, kinv_ref,
-    colsum, ohrow, ohcol, own_prod, chg,
+    values, vt, dang_in, start_in, x_ref, inv_ref, kinv_ref,
+    colsum, ohcol, own_prod, chg,
+    pk_own, pk_send, pk_recv, kg_ref, hot_own, hot_far, ohq,
     px_recv, pd_recv, col_send, col_recv, cs_recv, row_send, row_recv,
-    sc_send, sc_recv, ma_send, ma_recv,
+    sc_recv, ma_send, ma_recv,
     pr_send, pr_recv, sp_send, sp_recv, rs_send, rs_recv,
     rows_ref, cols_ref, count_ref,
     sem_in, sem_v,
@@ -50,7 +53,9 @@
     slots, edge, _ = values.shape
     blocks = x_ref.shape[0]
     halves = edge // 128
-    nchunk = slots // CHUNK
+    nchunk = slots // PIECE
+    early = nchunk // 2
+    cuts = [(sum(CUTS[:i]), n) for i, n in enumerate(CUTS)]
     f32, bf16 = jnp.float32, jnp.bfloat16
 
     def remote(src, dst, ss, rs, ll, rr, cc):
@@ -63,7 +68,7 @@
     in_x = pltpu.make_async_copy(start_hbm, start_in, sem_in.at[1])
     vcopies = [
         pltpu.make_async_copy(
-            values_hbm.at[pl.ds(k * CHUNK, CHUNK)], values.at[pl.ds(k * CHUNK, CHUNK)], sem_v.at[k]
+            values_hbm.at[pl.ds(k * PIECE, PIECE)], values.at[pl.ds(k * PIECE, PIECE)], sem_v.at[k]
         )
         for k in range(nchunk)
     ]
@@ -112,24 +117,30 @@
 
     eye = lax.broadcasted_iota(jnp.int32, (slots, slots), 0) == lax.broadcasted_iota(
         jnp.int32, (slots, slots), 1)
-    colv = jnp.sum(
-        jnp.where(eye, jnp.broadcast_to(cols_ref[...], (slots, slots)).astype(f32), 0.0),
-        axis=1, keepdims=True,
-    )
+
+    def upright(tab):
+        return jnp.sum(
+            jnp.where(eye, jnp.broadcast_to(tab, (slots, slots)), 0.0), axis=1, keepdims=True)
+
+    colv = upright(cols_ref[...].astype(f32))
     for d in range(nr):
         base = lax.rem(r - d + nr, nr) * blocks
         at = (lax.broadcasted_iota(jnp.int32, (slots, blocks), 1) + base).astype(f32)
         ohcol[d] = jnp.where(colv == at, 1.0, 0.0).astype(bf16)
 
     ones = jnp.ones((CHUNK, edge), bf16)
-    rid = lax.broadcasted_iota(jnp.int32, (CHUNK, edge), 0)
+    rid = lax.broadcasted_iota(jnp.int32, (PIECE, edge), 0)
 
     def column_sum(k):
         vcopies[k].wait()
-        acc = jnp.zeros((CHUNK, edge), f32)
-        for s in range(CHUNK):
-            acc = jnp.where(rid == s, dot(ones, values[k * CHUNK + s]), acc)
+        acc = jnp.zeros((PIECE, edge), f32)
+        for s in range(PIECE):
+            acc = jnp.where(rid == s, dot(ones, values[k * PIECE + s])[0:PIECE], acc)
         colsum[k] = acc
+
+    def transpose(k):
+        for s in range(k * PIECE, (k + 1) * PIECE):
+            vt[s] = values[s].T
 
     in_x.wait()
     in_d.wait()
@@ -147,6 +158,9 @@
     far_peers = [(dr, cc, d) for cc, d in far for dr in range(nr)]
     far_peers += [(dr, c, 0) for dr in range(1, nr)]
     sent = []
+
+    for k in range(1, nchunk - 1):
+        column_sum(k)
 
     pl.semaphore_wait(
         barrier, len(peers) + (l > 0).astype(jnp.int32) + (l < nl - 1).astype(jnp.int32))
@@ -163,7 +177,7 @@
         ])
     for cc, d in far:
         prow.append(remote(row_send, row_recv.at[d], row_ss.at[d], row_rs.at[d], l, r, cc))
-    for cp in px + pd + pc + prow + [q[0] for q in pcs]:
+    for cp in [cp for q in pcs for cp in q[:-1]] + px + pd + pc:
         cp.start()
 
     def spill_copies(t):
@@ -174,15 +188,16 @@
 
     spread = jnp.where((l == 0) | (l == nl - 1), 1.0, 0.5).astype(f32) * coupling
 
-    def send_spill(t, x):
-        sp_send[t] = (x * spread).astype(sp_send.dtype)
+    def send_spill(t, x, when):
+        if x is not None:
+            sp_send[t] = (x * spread).astype(sp_send.dtype)
         up, down = spill_copies(t)
 
-        @pl.when(l < nl - 1)
+        @pl.when((l < nl - 1) & when)
         def _():
             up.start()
 
-        @pl.when(l > 0)
+        @pl.when((l > 0) & when)
         def _():
             down.start()
 
@@ -196,24 +211,26 @@
         for t in range(ITERS):
             sp_recv[t, 1] = jnp.zeros((blocks, edge), sp_recv.dtype)
 
-    send_spill(0, x_ref[...])
-
-    for k in range(1, nchunk):
-        column_sum(k)
-        for q in pcs:
-            q[k].start()
-
-    def spread_sums(tab, sums, rr):
+    column_sum(nchunk - 1)
+    for q in pcs:
+        q[-1].start()
+    for k in range(early):
+        transpose(k)
+
+    def hot(tab, rr):
         at = (lax.broadcasted_iota(jnp.int32, (blocks, slots), 0) + rr * blocks).astype(f32)
-        oh = jnp.where(
+        return jnp.where(
             jnp.broadcast_to(tab[0:1, 0:slots], (blocks, slots)) == at, 1.0, 0.0).astype(bf16)
+
+    def spread_sums(oh, sums):
         hi, lo = split(sums.reshape(slots, edge))
         return dot(oh, hi) + dot(oh, lo)
 
     def piece(buf, h):
         return buf[pl.ds(h, blocks, stride=halves), :]
 
-    near = [spread_sums(col_send, colsum[...], lax.rem(r - d + nr, nr)) for d in range(nr)]
+    whose = [lax.rem(r - d + nr, nr) for d in range(nr)]
+    near = [spread_sums(hot(col_send, rr), colsum[...]) for rr in whose]
     for cp in px + pd + pc:
         cp.wait_recv()
     peer_x = {d: jnp.concatenate([piece(px_recv.at[d], h) for h in range(halves)], axis=1)
@@ -221,40 +238,90 @@
     keeps = {d: 1.0 - jnp.concatenate(
         [piece(pd_recv.at[d] if d else dang_in, h) for h in range(halves)], axis=1).astype(f32)
         for d in range(nr)}
+    hots = [[hot(col_recv[e], rr) for e in range(1, nr)] for rr in whose]
+    for e in range(nr):
+        tab = colv if e == 0 else upright(col_recv[e][0:1, 0:slots])
+        at = (lax.broadcasted_iota(jnp.int32, (slots, blocks), 1) + r * blocks).astype(f32)
+        ohq[e * slots : (e + 1) * slots] = jnp.where(tab == at, 1.0, 0.0).astype(bf16)
     for q in pcs:
         for cp in q:
             cp.wait_recv()
+    for cp in prow:
+        cp.start()
+    send_spill(0, x_ref[...], r >= 0)
     for d in range(nr):
         deg = near[d]
         for e in range(1, nr):
-            deg = deg + spread_sums(col_recv[e], cs_recv[e], lax.rem(r - d + nr, nr))
+            deg = deg + spread_sums(hots[d][e - 1], cs_recv[e])
         inv = 1.0 / (keeps[d] * deg + 1.0)
         kinv = keeps[d] * inv
         if d == 0:
             inv_ref[...] = inv
             kinv_ref[...] = kinv
         else:
-            sc_recv[0, d] = (peer_x[d] * kinv).astype(bf16)
-
-    def row_onehot(tab):
-        at = (lax.broadcasted_iota(jnp.int32, (blocks, slots), 0) + c * blocks).astype(f32)
-        return jnp.where(jnp.broadcast_to(tab[0:1, 0:slots], (blocks, slots)) == at,
-                         1.0, 0.0).astype(bf16)
-
-    def step(t):
-        x = x_ref[...]
-        scaled = (x * kinv_ref[...]).astype(bf16)
-        if t > 0:
-            sc_send[t] = scaled
-        sc = [
-            remote(sc_send.at[t], sc_recv.at[t, d], sc_ss.at[t, d], sc_rs.at[t, d],
+            sc_recv[d] = (peer_x[d] * kinv).astype(bf16)
+
+    def row_onehot(tabs):
+        tab = jnp.concatenate([tab[0:1, 0:slots] for tab in tabs], axis=1)
+        shape = (blocks, tab.shape[1])
+        at = (lax.broadcasted_iota(jnp.int32, shape, 0) + c * blocks).astype(f32)
+        return jnp.where(jnp.broadcast_to(tab, shape) == at, 1.0, 0.0).astype(bf16)
+
+    def pick_copies(t):
+        return [
+            remote(pk_send.at[t, d], pk_recv.at[t, d], sc_ss.at[t, d], sc_rs.at[t, d],
                    l, lax.rem(r + d, nr), c)
             for d in range(1, nr)
-            if t > 0
         ]
-        for cp in sc:
-            cp.start()
-        mass_own = jnp.sum(fold(x * inv_ref[...]), axis=0, keepdims=True)
+
+    def picks(t):
+        if t == 0:
+            acc = dot(ohcol[0], (x_ref[...] * kinv_ref[...]).astype(bf16))
+            for d in range(1, nr):
+                acc = acc + dot(ohcol[d], sc_recv[d])
+            return acc.astype(bf16)
+        acc = pk_own[...]
+        for d, cp in enumerate(pick_copies(t), 1):
+            cp.wait_recv()
+            acc = acc + pk_recv[t, d].astype(f32)
+        return acc.astype(bf16)
+
+    def products(t):
+        picked = picks(t)
+        if t > 0:
+            send_spill(t, None, lax.rem(r, 2) == 0)
+        def piece_copy(k, cc, d):
+            at, n = cuts[k]
+            return remote(
+                pr_send.at[t, pl.ds(at, n)], pr_recv.at[t, d, pl.ds(at, n)], pr_ss.at[t, d, k],
+                pr_rs.at[t, d, k], l, r, cc)
+
+        pr = []
+        for k, (at, n) in enumerate(cuts):
+            for at in range(at, at + n, PIECE):
+                base = at // CHUNK * CHUNK
+                lhs = picked[base : base + CHUNK]
+                acc = jnp.zeros((PIECE, edge), f32)
+                for s in range(PIECE):
+                    if t == 0 and at >= early * PIECE:
+                        res = lax.dot_general(
+                            lhs, values[at + s], (((1,), (1,)), ((), ())),
+                            preferred_element_type=f32)
+                    else:
+                        res = dot(lhs, vt[at + s])
+                    acc = jnp.where(rid == s, res[at - base : at - base + PIECE], acc)
+                own_prod[at : at + PIECE] = acc
+                pr_send[t, at : at + PIECE] = acc.astype(pr_send.dtype)
+            pr += [piece_copy(k, *to) for to in (far[:-1] if k < len(cuts) - 1 else far)]
+            for cp in pr[-len(far) + (k < len(cuts) - 1) :]:
+                cp.start()
+        for k in range(len(cuts) - 1):
+            pr.append(piece_copy(k, *far[-1]))
+            pr[-1].start()
+        sent.extend(pr)
+
+    def masses(t):
+        mass_own = jnp.sum(fold(x_ref[...] * inv_ref[...]), axis=0, keepdims=True)
         ma_send[t] = mass_own
         ma = []
         for i, (dr, cc, dc) in enumerate(far_peers):
@@ -263,43 +330,35 @@
                              ma_rs.at[t, slot], l, lax.rem(r + dr, nr), cc))
         for cp in ma:
             cp.start()
-
-        if t > 0:
-            send_spill(t, x)
-
-        picked = dot(ohcol[0], scaled)
-        for d in range(1, nr):
-            if t > 0:
-                sc[d - 1].wait_recv()
-            picked = picked + dot(ohcol[d], sc_recv[t, d])
-        picked = picked.astype(bf16)
-
-        pr = []
-        for k in range(nchunk):
-            lhs = picked[k * CHUNK : (k + 1) * CHUNK]
-            acc = jnp.zeros((CHUNK, edge), f32)
-            for s in range(CHUNK):
-                res = lax.dot_general(
-                    lhs, values[k * CHUNK + s], (((1,), (1,)), ((), ())),
-                    preferred_element_type=f32)
-                acc = jnp.where(rid == s, res, acc)
-            own_prod[k * CHUNK : (k + 1) * CHUNK] = acc
-            pr_send[t, k] = acc.astype(pr_send.dtype)
-            for cc, d in far:
-                cp = remote(pr_send.at[t, k], pr_recv.at[t, d, k], pr_ss.at[t, d, k],
-                            pr_rs.at[t, d, k], l, r, cc)
-                cp.start()
-                pr.append(cp)
-
+        sent.extend(ma)
+        return mass_own, ma
+
+    def note_change(t, diff):
+        part = jnp.sum(fold(jnp.abs(diff)), axis=0, keepdims=True)
+        lane = lax.broadcasted_iota(jnp.int32, (1, 128), 1)
+        old = chg[...] if t else jnp.zeros((1, 128), f32)
+        chg[...] = jnp.where(lane == t, jnp.sum(part, axis=1, keepdims=True), old)
+
+    def step(t, mass_own, ma):
+        products(t)
         if t == 0:
-            ohrow[0] = row_onehot(row_send)
+            for k in range(early, nchunk):
+                transpose(k)
             for cp in prow:
                 cp.wait_recv()
-            for d in range(1, nc):
-                ohrow[d] = row_onehot(row_recv[d])
+            for part, tabs in enumerate([[row_send], [row_recv.at[d] for d in range(1, nc)]]):
+                oh = row_onehot(tabs)
+                ref = hot_far if part else hot_own
+                ref[nr * slots :] = oh
+                ref[0 : nr * slots] = dot(ohq[...], oh).astype(bf16)
+            khi, klo = split(kinv_ref[...])
+            kg_ref[...] = dot(ohq[...], khi) + dot(ohq[...], klo)
 
         phi, plo = split(own_prod[...])
-        walk = dot(ohrow[0], phi) + dot(ohrow[0], plo)
+        last = t == ITERS - 1
+        npick = 0 if last else nr * slots
+        skip = nr * slots - npick
+        near_sum = dot(hot_own[skip:], phi) + dot(hot_own[skip:], plo)
 
         up, down = spill_copies(t)
 
@@ -317,31 +376,46 @@
             cp.wait_recv()
         for i in range(len(peers)):
             mass = mass + ma_recv[t, i]
-        rest = damping * ((1.0 - coupling) * (jnp.sum(mass) / nodes) + arrive) + (1.0 - damping)
-
+        flat = damping * (1.0 - coupling) * (jnp.sum(mass) / nodes) + (1.0 - damping)
+        rest = damping * arrive + flat
+        if not last:
+            restg = damping * (dot(ohq[...], sp_recv[t, 0]) + dot(ohq[...], sp_recv[t, 1])) + flat
+
+        gain = damping * (1.0 - coupling)
+        if not last:
+            near_pick = gain * near_sum[0:npick] + restg
+        near_walk = gain * near_sum[npick:] + rest
         for d in range(1, nc):
-            for k in range(nchunk):
-                remote(pr_send.at[t, k], pr_recv.at[t, d, k], pr_ss.at[t, d, k], pr_rs.at[t, d, k], l, r, lax.rem(c + d, nc)).wait_recv()
-            got = pr_recv[t, d].reshape(slots, edge)
-            if got.dtype == bf16:
-                walk = walk + dot(ohrow[d], got)
-            else:
-                ghi, glo = split(got)
-                walk = walk + dot(ohrow[d], ghi) + dot(ohrow[d], glo)
-        updated = damping * (1.0 - coupling) * walk + rest
+            for k, (at, n) in enumerate(cuts):
+                remote(pr_send.at[t, pl.ds(at, n)], pr_recv.at[t, d, pl.ds(at, n)],
+                       pr_ss.at[t, d, k], pr_rs.at[t, d, k],
+                       l, r, lax.rem(c + d, nc)).wait_recv()
+        far_sum = dot(hot_far[skip:], pr_recv[t, 1:nc].reshape((nc - 1) * slots, edge))
+        if not last:
+            pk = kg_ref[...] * (gain * far_sum[0:npick] + near_pick)
+            for d in range(1, nr):
+                pk_send[t + 1, d] = pk[d * slots : (d + 1) * slots].astype(bf16)
+            pk_own[...] = pk[0:slots].astype(bf16).astype(f32)
+            cps = pick_copies(t + 1)
+            for cp in cps:
+                cp.start()
+            sent.extend(cps)
+        x = x_ref[...]
+        updated = gain * far_sum[npick:] + near_walk
         x_ref[...] = updated
-        chg[t] = fold(jnp.abs(updated - x))
-
-        sent.extend(sc + ma + pr)
-
+        if last:
+            note_change(t, updated - x)
+            return None
+        send_spill(t + 1, updated, lax.rem(r, 2) == 1)
+        out = masses(t + 1)
+        note_change(t, updated - x)
+        return out
+
+    carry = masses(0)
     for t in range(ITERS):
-        step(t)
-
-    lane = lax.broadcasted_iota(jnp.int32, (1, 128), 1)
-    changes = jnp.zeros((1, 128), f32)
-    for t in range(ITERS):
-        changes = jnp.where(lane == t, jnp.sum(chg[t]), changes)
-    rs_send[...] = changes
+        carry = step(t, *carry)
+
+    rs_send[...] = chg[...]
     rs = []
     for dr, cc, dc in far_peers:
         i = dr * nc + dc - 1
@@ -389,7 +463,7 @@
     nl, nr, nc = (lax.axis_size(a) for a in ("layer", "row", "col"))
     slots, edge = block_values.shape[3], block_values.shape[-1]
     blocks = span // edge
-    nchunk = slots // CHUNK
+    nchunk = slots // PIECE
     nodes = nr * nc * span
     npeer = nr * nc - 1
     f32, bf16 = jnp.float32, jnp.bfloat16
@@ -397,16 +471,19 @@
     big = (blocks, edge)
     PT, ST = bf16, bf16
     scratch = [
-        vm((slots, edge, edge), bf16), vm((span // 128, 128), jnp.int32), vm((span // 128, 128), f32),
+        vm((slots, edge, edge), bf16), vm((slots, edge, edge), bf16), vm((span // 128, 128), jnp.int32), vm((span // 128, 128), f32),
         vm(big, f32), vm(big, f32), vm(big, f32),
-        vm((nchunk, CHUNK, edge), f32), vm((nc, blocks, slots), bf16), vm((nr, slots, blocks), bf16),
-        vm((slots, edge), f32), vm((ITERS, 8, 128), f32),
+        vm((nchunk, PIECE, edge), f32), vm((nr, slots, blocks), bf16),
+        vm((slots, edge), f32), vm((1, 128), f32),
+        vm((slots, edge), f32), vm((ITERS, nr, slots, edge), bf16), vm((ITERS, nr, slots, edge), bf16),
+        vm((nr * slots, edge), f32), vm((nr * slots + blocks, slots), bf16),
+        vm((nr * slots + blocks, (nc - 1) * slots), bf16), vm((nr * slots, blocks), bf16),
         vm((nr, span // 128, 128), f32), vm((nr, span // 128, 128), jnp.int32),
-        vm((8, 128), f32), vm((nr, 8, 128), f32), vm((nr, nchunk, CHUNK, edge), f32),
+        vm((8, 128), f32), vm((nr, 8, 128), f32), vm((nr, nchunk, PIECE, edge), f32),
         vm((8, 128), f32), vm((nc, 8, 128), f32),
-        vm((ITERS,) + big, bf16), vm((ITERS, nr) + big, bf16),
+        vm((nr,) + big, bf16),
         vm((ITERS, 1, 128), f32), vm((ITERS, npeer, 1, 128), f32),
-        vm((ITERS, nchunk, CHUNK, edge), PT), vm((ITERS, nc, nchunk, CHUNK, edge), PT),
+        vm((ITERS, slots, edge), PT), vm((ITERS, nc, slots, edge), PT),
         vm((ITERS,) + big, ST), vm((ITERS, 2) + big, ST),
         vm((1, 128), f32), vm((npeer, 1, 128), f32),
         vm((1, slots), jnp.int32), vm((1, slots), jnp.int32), vm((1, 1), jnp.int32),
@@ -416,7 +493,7 @@
         dma((nr,)), dma((nr,)), dma((nr,)), dma((nr,)), dma((nr,)), dma((nr,)),
         dma((nr, nchunk)), dma((nr, nchunk)), dma((nc,)), dma((nc,)),
         dma((ITERS, nr)), dma((ITERS, nr)), dma((ITERS, npeer)), dma((ITERS, npeer)),
-        dma((ITERS, nc, nchunk)), dma((ITERS, nc, nchunk)),
+        dma((ITERS, nc, len(CUTS))), dma((ITERS, nc, len(CUTS))),
         dma((ITERS, 2)), dma((ITERS, 2)), dma((npeer,)), dma((npeer,)),
     ]
     hbm = pl.BlockSpec(memory_space=pltpu.HBM)

time: 28.5 us -> 27.1 us (0.951)
  Pallas kernels: 27.1 us -> 25.6 us
    pallas_call x1, Pallas kernels: 26.5 us -> 25 us  [local(): pl.pallas_call(functools.partial(scoped, sems, nl, nr, nc, nodes), out_sh...]
where the time goes in v2:
time: 27.1 us; the launch traced here: 26.9 us
  Pallas kernels  25.6 us (94%)
  between operations  1.28 us (5%)
    pallas_call x1, Pallas kernels, local(): pl.pallas_call(functools.partial(scoped, sems, nl, nr, nc, nodes), out_sh...  25 us
    pallas_call x1, Pallas kernels, local(): pl.pallas_call(finish, out_shape=(jax.ShapeDtypeStruct((span // 128, 128)...  0.64 us

profile of v2, /device:TPU:0, one launch (start us, length us, event | category | flops | bytes accessed | tf_op | source)
XLA Modules:
  0.0 26.9 jit_solution(13825722228232587133)
XLA Ops:
  1.3 25.0 %shard_map.77 = (f32[128,128]{1,0:T(8,128)S(1)}, f32[1,128]{1,0:T(1,128)S(1)}) custom-call(bf16[32,256,256]{2,1,0:T(8,128)(2,1)} %bitcast.9, s32[1,32]{1,0:T(1,128)} %bitcast.12, s32[1,32]{1,0:T(1,128)} %bitcast.13, s32[1,1]{1,0:T(1,128)} %bitcast.8.args_3_, s32[128,128]{1,0:T(8,128)} %bitcast.10, f32[128,128]{1,0:T(8,128)} %bitcast.11), custom_call_target="tpu_custom_call" | custom-call | tf_op jit(solution)/shard_map/pallas_call | solution.py:501
  26.3 0.6 %shard_map.78 = (f32[128,128]{1,0:T(8,128)}, f32[1,3]{1,0:T(1,128)}) custom-call(f32[128,128]{1,0:T(8,128)S(1)} %get-tuple-element.6.ranks_in, f32[1,128]{1,0:T(1,128)S(1)} %get-tuple-element.7.resid_in), custom_call_target="tpu_custom_call" | custom-call | tf_op jit(solution)/shard_map/pallas_call | solution.py:519

commit v3 on v2

--- a/solution.py
+++ b/solution.py
@@ -39,7 +39,7 @@
     values_hbm, rows_hbm, cols_hbm, count_hbm, dang_hbm, start_hbm,
     ranks_ref, resid_ref,
     values, vt, dang_in, start_in, x_ref, inv_ref, kinv_ref,
-    colsum, ohcol, own_prod, chg,
+    colsum, ohcol, own_prod, diff, chg,
     pk_own, pk_send, pk_recv, kg_ref, hot_own, hot_far, ohq,
     px_recv, pd_recv, col_send, col_recv, cs_recv, row_send, row_recv,
     sc_recv, ma_send, ma_recv,
@@ -47,6 +47,7 @@
     rows_ref, cols_ref, count_ref,
     sem_in, sem_v,
     px_ss, px_rs, pd_ss, pd_rs, col_ss, col_rs, cs_ss, cs_rs, row_ss, row_rs, sc_ss, sc_rs, ma_ss, ma_rs,
+    ready,
     pr_ss, pr_rs, sp_ss, sp_rs, rs_ss, rs_rs,
 ):
     l, r, c = (lax.axis_index(a) for a in ("layer", "row", "col"))
@@ -86,34 +87,29 @@
 
     peers = [(dr, dc) for dr in range(nr) for dc in range(nc) if (dr, dc) != (0, 0)]
     barrier = pltpu.get_barrier_semaphore()
-    for dr, dc in peers:
-        pl.semaphore_signal(
-            barrier, inc=1,
-            device_id=(l, lax.rem(r + dr, nr), lax.rem(c + dc, nc)),
-            device_id_type=pl.DeviceIdType.MESH,
-        )
-
-    @pl.when(l > 0)
-    def _():
-        pl.semaphore_signal(
-            barrier, inc=1, device_id=(l - 1, r, c), device_id_type=pl.DeviceIdType.MESH)
+    def tell(sem, *to):
+        pl.semaphore_signal(sem, inc=1, device_id=to, device_id_type=pl.DeviceIdType.MESH)
+
+    for d in range(1, nr):
+        tell(barrier, l, lax.rem(r + d, nr), c)
+    for d in range(1, nc):
+        @pl.when(c + d < nc)
+        def _():
+            for rr in range(nr):
+                tell(barrier, l, rr, c + d)
 
     @pl.when(l < nl - 1)
     def _():
-        pl.semaphore_signal(
-            barrier, inc=1, device_id=(l + 1, r, c), device_id_type=pl.DeviceIdType.MESH)
+        tell(barrier, l + 1, r, c)
 
     for cp in small:
         cp.wait()
     live = lax.broadcasted_iota(jnp.int32, (1, slots), 1) < count_ref[...]
     rows = jnp.where(live, rows_ref[...], -1)
     cols = jnp.where(live, cols_ref[...], -1)
-    row_send[...] = jnp.broadcast_to(
-        jnp.concatenate([rows, jnp.full((1, 128 - slots), -1, jnp.int32)], axis=1), (8, 128)
-    ).astype(f32)
-    col_send[...] = jnp.broadcast_to(
-        jnp.concatenate([cols, jnp.full((1, 128 - slots), -1, jnp.int32)], axis=1), (8, 128)
-    ).astype(f32)
+    pad = jnp.full((1, 128 - slots), -1, jnp.int32)
+    row_send[...] = jnp.concatenate([rows, pad], axis=1).astype(f32)
+    col_send[...] = jnp.concatenate([cols, pad], axis=1).astype(f32)
 
     eye = lax.broadcasted_iota(jnp.int32, (slots, slots), 0) == lax.broadcasted_iota(
         jnp.int32, (slots, slots), 1)
@@ -141,6 +137,17 @@
     def transpose(k):
         for s in range(k * PIECE, (k + 1) * PIECE):
             vt[s] = values[s].T
+
+    pl.semaphore_wait(barrier, nr - 1 + nr * c + (l > 0).astype(jnp.int32))
+    for d in range(1, nc):
+        @pl.when(c >= d)
+        def _():
+            for rr in range(nr):
+                tell(ready.at[0], l, rr, c - d)
+
+    @pl.when(l > 0)
+    def _():
+        tell(ready.at[1], l - 1, r, c)
 
     in_x.wait()
     in_d.wait()
@@ -158,12 +165,6 @@
     far_peers = [(dr, cc, d) for cc, d in far for dr in range(nr)]
     far_peers += [(dr, c, 0) for dr in range(1, nr)]
     sent = []
-
-    for k in range(1, nchunk - 1):
-        column_sum(k)
-
-    pl.semaphore_wait(
-        barrier, len(peers) + (l > 0).astype(jnp.int32) + (l < nl - 1).astype(jnp.int32))
 
     px, pd, pc, pcs, prow = [], [], [], [], []
     for d in range(1, nr):
@@ -177,8 +178,16 @@
         ])
     for cc, d in far:
         prow.append(remote(row_send, row_recv.at[d], row_ss.at[d], row_rs.at[d], l, r, cc))
-    for cp in [cp for q in pcs for cp in q[:-1]] + px + pd + pc:
+    for cp in px + pd + pc + [q[0] for q in pcs]:
         cp.start()
+
+    def start_where(pairs):
+        for cp, cond in pairs:
+            @pl.when(cond)
+            def _():
+                cp.start()
+
+    start_where([(cp, cc < c) for cp, (cc, _) in zip(prow, far)])
 
     def spill_copies(t):
         return (
@@ -211,9 +220,10 @@
         for t in range(ITERS):
             sp_recv[t, 1] = jnp.zeros((blocks, edge), sp_recv.dtype)
 
-    column_sum(nchunk - 1)
-    for q in pcs:
-        q[-1].start()
+    for k in range(1, nchunk):
+        column_sum(k)
+        for q in pcs:
+            q[k].start()
     for k in range(early):
         transpose(k)
 
@@ -246,8 +256,10 @@
     for q in pcs:
         for cp in q:
             cp.wait_recv()
-    for cp in prow:
-        cp.start()
+    @pl.when(l < nl - 1)
+    def _():
+        pl.semaphore_wait(ready.at[1], 1)
+
     send_spill(0, x_ref[...], r >= 0)
     for d in range(nr):
         deg = near[d]
@@ -286,7 +298,7 @@
             acc = acc + pk_recv[t, d].astype(f32)
         return acc.astype(bf16)
 
-    def products(t):
+    def products(t, ma):
         picked = picks(t)
         if t > 0:
             send_spill(t, None, lax.rem(r, 2) == 0)
@@ -312,9 +324,22 @@
                     acc = jnp.where(rid == s, res[at - base : at - base + PIECE], acc)
                 own_prod[at : at + PIECE] = acc
                 pr_send[t, at : at + PIECE] = acc.astype(pr_send.dtype)
+            if t == 0 and k == 0:
+                @pl.when(c < nc - 1)
+                def _():
+                    pl.semaphore_wait(ready.at[0], nr * (nc - 1 - c))
+
+                start_where([(cp, cc > c) for cp, (cc, _) in zip(prow, far)])
+                start_where([(cp, cc > c) for cp, (_, cc, _) in zip(ma, far_peers)])
             pr += [piece_copy(k, *to) for to in (far[:-1] if k < len(cuts) - 1 else far)]
             for cp in pr[-len(far) + (k < len(cuts) - 1) :]:
                 cp.start()
+            if t > 0 and k == 0:
+                @pl.when(lax.rem(r, 2) == 0)
+                def _():
+                    for cp in ma:
+                        cp.start()
+
         for k in range(len(cuts) - 1):
             pr.append(piece_copy(k, *far[-1]))
             pr[-1].start()
@@ -328,19 +353,27 @@
             slot = dr * nc + dc - 1
             ma.append(remote(ma_send.at[t], ma_recv.at[t, slot], ma_ss.at[t, slot],
                              ma_rs.at[t, slot], l, lax.rem(r + dr, nr), cc))
-        for cp in ma:
-            cp.start()
+        if t == 0:
+            start_where([(cp, cc <= c) for cp, (_, cc, _) in zip(ma, far_peers)])
+        else:
+            @pl.when(lax.rem(r, 2) == 1)
+            def _():
+                for cp in ma:
+                    cp.start()
+
         sent.extend(ma)
         return mass_own, ma
 
-    def note_change(t, diff):
-        part = jnp.sum(fold(jnp.abs(diff)), axis=0, keepdims=True)
+    def note_change(t):
+        part = jnp.sum(diff[t], axis=0, keepdims=True)
         lane = lax.broadcasted_iota(jnp.int32, (1, 128), 1)
         old = chg[...] if t else jnp.zeros((1, 128), f32)
         chg[...] = jnp.where(lane == t, jnp.sum(part, axis=1, keepdims=True), old)
 
     def step(t, mass_own, ma):
-        products(t)
+        products(t, ma)
+        if t > 0:
+            note_change(t - 1)
         if t == 0:
             for k in range(early, nchunk):
                 transpose(k)
@@ -403,13 +436,12 @@
         x = x_ref[...]
         updated = gain * far_sum[npick:] + near_walk
         x_ref[...] = updated
+        diff[t] = fold(jnp.abs(updated - x))
         if last:
-            note_change(t, updated - x)
+            note_change(t)
             return None
         send_spill(t + 1, updated, lax.rem(r, 2) == 1)
-        out = masses(t + 1)
-        note_change(t, updated - x)
-        return out
+        return masses(t + 1)
 
     carry = masses(0)
     for t in range(ITERS):
@@ -474,13 +506,13 @@
         vm((slots, edge, edge), bf16), vm((slots, edge, edge), bf16), vm((span // 128, 128), jnp.int32), vm((span // 128, 128), f32),
         vm(big, f32), vm(big, f32), vm(big, f32),
         vm((nchunk, PIECE, edge), f32), vm((nr, slots, blocks), bf16),
-        vm((slots, edge), f32), vm((1, 128), f32),
+        vm((slots, edge), f32), vm((ITERS, 8, 128), f32), vm((1, 128), f32),
         vm((slots, edge), f32), vm((ITERS, nr, slots, edge), bf16), vm((ITERS, nr, slots, edge), bf16),
         vm((nr * slots, edge), f32), vm((nr * slots + blocks, slots), bf16),
         vm((nr * slots + blocks, (nc - 1) * slots), bf16), vm((nr * slots, blocks), bf16),
         vm((nr, span // 128, 128), f32), vm((nr, span // 128, 128), jnp.int32),
-        vm((8, 128), f32), vm((nr, 8, 128), f32), vm((nr, nchunk, PIECE, edge), f32),
-        vm((8, 128), f32), vm((nc, 8, 128), f32),
+        vm((1, 128), f32), vm((nr, 1, 128), f32), vm((nr, nchunk, PIECE, edge), f32),
+        vm((1, 128), f32), vm((nc, 1, 128), f32),
         vm((nr,) + big, bf16),
         vm((ITERS, 1, 128), f32), vm((ITERS, npeer, 1, 128), f32),
         vm((ITERS, slots, edge), PT), vm((ITERS, nc, slots, edge), PT),
@@ -493,6 +525,7 @@
         dma((nr,)), dma((nr,)), dma((nr,)), dma((nr,)), dma((nr,)), dma((nr,)),
         dma((nr, nchunk)), dma((nr, nchunk)), dma((nc,)), dma((nc,)),
         dma((ITERS, nr)), dma((ITERS, nr)), dma((ITERS, npeer)), dma((ITERS, npeer)),
+        pltpu.SemaphoreType.REGULAR((2,)),
         dma((ITERS, nc, len(CUTS))), dma((ITERS, nc, len(CUTS))),
         dma((ITERS, 2)), dma((ITERS, 2)), dma((npeer,)), dma((npeer,)),
     ]

time: 27.1 us -> 27 us (level)
  no operation moved by 1% of the time
where the time goes in v3:
time: 27 us; the launch traced here: 26.8 us
  Pallas kernels  25.6 us (95%)
  between operations  1.28 us (5%)
    pallas_call x1, Pallas kernels, local(): pl.pallas_call(functools.partial(scoped, sems, nl, nr, nc, nodes), out_sh...  24.9 us
    pallas_call x1, Pallas kernels, local(): pl.pallas_call(finish, out_shape=(jax.ShapeDtypeStruct((span // 128, 128)...  0.64 us

profile of v3, /device:TPU:0, one launch (start us, length us, event | category | flops | bytes accessed | tf_op | source)
XLA Modules:
  0.0 26.8 jit_solution(10033149847978828740)
XLA Ops:
  1.3 24.9 %shard_map.77 = (f32[128,128]{1,0:T(8,128)S(1)}, f32[1,128]{1,0:T(1,128)S(1)}) custom-call(bf16[32,256,256]{2,1,0:T(8,128)(2,1)} %bitcast.9, s32[1,32]{1,0:T(1,128)} %bitcast.12, s32[1,32]{1,0:T(1,128)} %bitcast.13, s32[1,1]{1,0:T(1,128)} %bitcast.8.args_3_, s32[128,128]{1,0:T(8,128)} %bitcast.10, f32[128,128]{1,0:T(8,128)} %bitcast.11), custom_call_target="tpu_custom_call" | custom-call | tf_op jit(solution)/shard_map/pallas_call | solution.py:534
  26.2 0.6 %shard_map.78 = (f32[128,128]{1,0:T(8,128)}, f32[1,3]{1,0:T(1,128)}) custom-call(f32[128,128]{1,0:T(8,128)S(1)} %get-tuple-element.6.ranks_in, f32[1,128]{1,0:T(1,128)S(1)} %get-tuple-element.7.resid_in), custom_call_target="tpu_custom_call" | custom-call | tf_op jit(solution)/shard_map/pallas_call | solution.py:552

commit v4 on v3

--- a/solution.py
+++ b/solution.py
@@ -39,6 +39,7 @@
     values_hbm, rows_hbm, cols_hbm, count_hbm, dang_hbm, start_hbm,
     ranks_ref, resid_ref,
     values, vt, dang_in, start_in, x_ref, inv_ref, kinv_ref,
+    kg_pair, kinv_pair, hot_pair, rowp_recv, pp_recv, rg_send, rg_recv,
     colsum, ohcol, own_prod, diff, chg,
     pk_own, pk_send, pk_recv, kg_ref, hot_own, hot_far, ohq,
     px_recv, pd_recv, col_send, col_recv, cs_recv, row_send, row_recv,
@@ -47,7 +48,7 @@
     rows_ref, cols_ref, count_ref,
     sem_in, sem_v,
     px_ss, px_rs, pd_ss, pd_rs, col_ss, col_rs, cs_ss, cs_rs, row_ss, row_rs, sc_ss, sc_rs, ma_ss, ma_rs,
-    ready,
+    ready, rowp_ss, rowp_rs, pp_ss, pp_rs, rg_ss, rg_rs,
     pr_ss, pr_rs, sp_ss, sp_rs, rs_ss, rs_rs,
 ):
     l, r, c = (lax.axis_index(a) for a in ("layer", "row", "col"))
@@ -55,7 +56,11 @@
     blocks = x_ref.shape[0]
     halves = edge // 128
     nchunk = slots // PIECE
-    early = nchunk // 2
+    early = nchunk * 3 // 4
+    gives = lax.rem(r, 2) == 0
+    takes = lax.rem(r, 2) == 1
+    mate = lax.rem(r + 1, nr)
+    gain = damping * (1.0 - coupling)
     cuts = [(sum(CUTS[:i]), n) for i, n in enumerate(CUTS)]
     f32, bf16 = jnp.float32, jnp.bfloat16
 
@@ -188,6 +193,17 @@
                 cp.start()
 
     start_where([(cp, cc < c) for cp, (cc, _) in zip(prow, far)])
+    everyone = far + [(c, 0)]
+    mate_rows = [
+        remote(row_send, rowp_recv.at[d], rowp_ss.at[d], rowp_rs.at[d], l, mate, cc)
+        for cc, d in everyone
+    ]
+    mate_prods = [
+        remote(pr_send.at[0], pp_recv.at[d], pp_ss.at[d], pp_rs.at[d], l, mate, cc)
+        for cc, d in everyone
+    ]
+    mate_rest = remote(rg_send, rg_recv, rg_ss.at[0], rg_rs.at[0], l, mate, c)
+    start_where([(cp, gives & (cc <= c)) for cp, (cc, _) in zip(mate_rows, everyone)])
 
     def spill_copies(t):
         return (
@@ -272,6 +288,8 @@
             kinv_ref[...] = kinv
         else:
             sc_recv[d] = (peer_x[d] * kinv).astype(bf16)
+            if d == 1:
+                kinv_pair[...] = kinv
 
     def row_onehot(tabs):
         tab = jnp.concatenate([tab[0:1, 0:slots] for tab in tabs], axis=1)
@@ -293,8 +311,21 @@
                 acc = acc + dot(ohcol[d], sc_recv[d])
             return acc.astype(bf16)
         acc = pk_own[...]
+        if t == 1:
+            @pl.when(takes)
+            def _():
+                for cp in mate_prods + [mate_rest]:
+                    cp.wait_recv()
+                pw = dot(hot_pair[...], pp_recv[...].reshape(nc * slots, edge))
+                pk_recv[1, 1] = (kg_pair[...] * (gain * pw + rg_recv[...])).astype(bf16)
+
         for d, cp in enumerate(pick_copies(t), 1):
-            cp.wait_recv()
+            if t == 1 and d == 1:
+                @pl.when(gives)
+                def _():
+                    cp.wait_recv()
+            else:
+                cp.wait_recv()
             acc = acc + pk_recv[t, d].astype(f32)
         return acc.astype(bf16)
 
@@ -330,20 +361,21 @@
                     pl.semaphore_wait(ready.at[0], nr * (nc - 1 - c))
 
                 start_where([(cp, cc > c) for cp, (cc, _) in zip(prow, far)])
+                start_where([(cp, gives & (cc > c)) for cp, (cc, _) in zip(mate_rows, everyone)])
                 start_where([(cp, cc > c) for cp, (_, cc, _) in zip(ma, far_peers)])
             pr += [piece_copy(k, *to) for to in (far[:-1] if k < len(cuts) - 1 else far)]
             for cp in pr[-len(far) + (k < len(cuts) - 1) :]:
                 cp.start()
-            if t > 0 and k == 0:
-                @pl.when(lax.rem(r, 2) == 0)
-                def _():
-                    for cp in ma:
-                        cp.start()
-
         for k in range(len(cuts) - 1):
             pr.append(piece_copy(k, *far[-1]))
             pr[-1].start()
         sent.extend(pr)
+        if t == 0:
+            @pl.when(gives)
+            def _():
+                for cp in mate_prods:
+                    cp.start()
+
 
     def masses(t):
         mass_own = jnp.sum(fold(x_ref[...] * inv_ref[...]), axis=0, keepdims=True)
@@ -356,11 +388,8 @@
         if t == 0:
             start_where([(cp, cc <= c) for cp, (_, cc, _) in zip(ma, far_peers)])
         else:
-            @pl.when(lax.rem(r, 2) == 1)
-            def _():
-                for cp in ma:
-                    cp.start()
-
+            for cp in ma:
+                cp.start()
         sent.extend(ma)
         return mass_own, ma
 
@@ -384,6 +413,15 @@
                 ref = hot_far if part else hot_own
                 ref[nr * slots :] = oh
                 ref[0 : nr * slots] = dot(ohq[...], oh).astype(bf16)
+            @pl.when(takes)
+            def _():
+                for cp in mate_rows:
+                    cp.wait_recv()
+                oh = row_onehot([rowp_recv.at[d] for d in range(nc)])
+                hot_pair[...] = dot(ohcol[1], oh).astype(bf16)
+                phi, plo = split(kinv_pair[...])
+                kg_pair[...] = dot(ohcol[1], phi) + dot(ohcol[1], plo)
+
             khi, klo = split(kinv_ref[...])
             kg_ref[...] = dot(ohq[...], khi) + dot(ohq[...], klo)
 
@@ -414,7 +452,13 @@
         if not last:
             restg = damping * (dot(ohq[...], sp_recv[t, 0]) + dot(ohq[...], sp_recv[t, 1])) + flat
 
-        gain = damping * (1.0 - coupling)
+        if t == 0:
+            rg_send[...] = restg[(nr - 1) * slots :]
+
+            @pl.when(gives)
+            def _():
+                mate_rest.start()
+
         if not last:
             near_pick = gain * near_sum[0:npick] + restg
         near_walk = gain * near_sum[npick:] + rest
@@ -430,6 +474,9 @@
                 pk_send[t + 1, d] = pk[d * slots : (d + 1) * slots].astype(bf16)
             pk_own[...] = pk[0:slots].astype(bf16).astype(f32)
             cps = pick_copies(t + 1)
+            if t == 0:
+                start_where([(cps[0], takes)])
+                cps = cps[1:]
             for cp in cps:
                 cp.start()
             sent.extend(cps)
@@ -459,6 +506,16 @@
         ranks_ref[pl.ds(h, blocks, stride=halves), :] = x_ref[:, h * 128 : (h + 1) * 128]
     for cp in px + pd + pc + prow + [e for q in pcs for e in q] + sent:
         cp.wait_send()
+
+    @pl.when(gives)
+    def _():
+        for cp in mate_rows + mate_prods + [mate_rest]:
+            cp.wait_send()
+
+    @pl.when(takes)
+    def _():
+        pick_copies(1)[0].wait_send()
+
     ups = [spill_copies(t) for t in range(ITERS)]
 
     @pl.when(l < nl - 1)
@@ -505,6 +562,8 @@
     scratch = [
         vm((slots, edge, edge), bf16), vm((slots, edge, edge), bf16), vm((span // 128, 128), jnp.int32), vm((span // 128, 128), f32),
         vm(big, f32), vm(big, f32), vm(big, f32),
+        vm((slots, edge), f32), vm(big, f32), vm((slots, nc * slots), bf16), vm((nc, 1, 128), f32),
+        vm((nc, slots, edge), PT), vm((slots, edge), f32), vm((slots, edge), f32),
         vm((nchunk, PIECE, edge), f32), vm((nr, slots, blocks), bf16),
         vm((slots, edge), f32), vm((ITERS, 8, 128), f32), vm((1, 128), f32),
         vm((slots, edge), f32), vm((ITERS, nr, slots, edge), bf16), vm((ITERS, nr, slots, edge), bf16),
@@ -526,6 +585,7 @@
         dma((nr, nchunk)), dma((nr, nchunk)), dma((nc,)), dma((nc,)),
         dma((ITERS, nr)), dma((ITERS, nr)), dma((ITERS, npeer)), dma((ITERS, npeer)),
         pltpu.SemaphoreType.REGULAR((2,)),
+        dma((nc,)), dma((nc,)), dma((nc,)), dma((nc,)), dma((1,)), dma((1,)),
         dma((ITERS, nc, len(CUTS))), dma((ITERS, nc, len(CUTS))),
         dma((ITERS, 2)), dma((ITERS, 2)), dma((npeer,)), dma((npeer,)),
     ]

time: 27 us -> 26.7 us (0.989)
  Pallas kernels: 25.6 us -> 25.3 us
    pallas_call x1, Pallas kernels: 24.9 us -> 24.6 us  [local(): pl.pallas_call(functools.partial(scoped, sems, nl, nr, nc, nodes), out_sh...]
where the time goes in v4:
time: 26.7 us; the launch traced here: 26.6 us
  Pallas kernels  25.3 us (95%)
  between operations  1.28 us (5%)
    pallas_call x1, Pallas kernels, local(): pl.pallas_call(functools.partial(scoped, sems, nl, nr, nc, nodes), out_sh...  24.6 us
    pallas_call x1, Pallas kernels, local(): pl.pallas_call(finish, out_shape=(jax.ShapeDtypeStruct((span // 128, 128)...  0.64 us

profile of v4, /device:TPU:0, one launch (start us, length us, event | category | flops | bytes accessed | tf_op | source)
XLA Modules:
  0.0 26.6 jit_solution(9266623951378317249)
XLA Ops:
  1.3 24.6 %shard_map.77 = (f32[128,128]{1,0:T(8,128)S(1)}, f32[1,128]{1,0:T(1,128)S(1)}) custom-call(bf16[32,256,256]{2,1,0:T(8,128)(2,1)} %bitcast.9, s32[1,32]{1,0:T(1,128)} %bitcast.12, s32[1,32]{1,0:T(1,128)} %bitcast.13, s32[1,1]{1,0:T(1,128)} %bitcast.8.args_3_, s32[128,128]{1,0:T(8,128)} %bitcast.10, f32[128,128]{1,0:T(8,128)} %bitcast.11), custom_call_target="tpu_custom_call" | custom-call | tf_op jit(solution)/shard_map/pallas_call | solution.py:594
  25.9 0.6 %shard_map.78 = (f32[128,128]{1,0:T(8,128)}, f32[1,3]{1,0:T(1,128)}) custom-call(f32[128,128]{1,0:T(8,128)S(1)} %get-tuple-element.6.ranks_in, f32[1,128]{1,0:T(1,128)S(1)} %get-tuple-element.7.resid_in), custom_call_target="tpu_custom_call" | custom-call | tf_op jit(solution)/shard_map/pallas_call | solution.py:612

commit v5 on v4

--- a/solution.py
+++ b/solution.py
@@ -331,8 +331,8 @@
 
     def products(t, ma):
         picked = picks(t)
-        if t > 0:
-            send_spill(t, None, lax.rem(r, 2) == 0)
+        if t > 1:
+            send_spill(t, None, gives)
         def piece_copy(k, cc, d):
             at, n = cuts[k]
             return remote(
@@ -373,7 +373,7 @@
         if t == 0:
             @pl.when(gives)
             def _():
-                for cp in mate_prods:
+                for cp in mate_prods[-1:] + mate_prods[:-1]:
                     cp.start()
 
 
@@ -487,8 +487,9 @@
         if last:
             note_change(t)
             return None
-        send_spill(t + 1, updated, lax.rem(r, 2) == 1)
-        return masses(t + 1)
+        out = masses(t + 1)
+        send_spill(t + 1, updated, takes if t else r >= 0)
+        return out
 
     carry = masses(0)
     for t in range(ITERS):

time: 26.7 us -> 26.7 us (level)
  no operation moved by 1% of the time
where the time goes in v5:
time: 26.7 us; the launch traced here: 26.5 us
  Pallas kernels  25.3 us (95%)
  between operations  1.28 us (5%)
    pallas_call x1, Pallas kernels, local(): pl.pallas_call(functools.partial(scoped, sems, nl, nr, nc, nodes), out_sh...  24.6 us
    pallas_call x1, Pallas kernels, local(): pl.pallas_call(finish, out_shape=(jax.ShapeDtypeStruct((span // 128, 128)...  0.64 us

profile of v5, /device:TPU:0, one launch (start us, length us, event | category | flops | bytes accessed | tf_op | source)
XLA Modules:
  0.0 26.5 jit_solution(14009944001098077151)
XLA Ops:
  1.3 24.6 %shard_map.77 = (f32[128,128]{1,0:T(8,128)S(1)}, f32[1,128]{1,0:T(1,128)S(1)}) custom-call(bf16[32,256,256]{2,1,0:T(8,128)(2,1)} %bitcast.9, s32[1,32]{1,0:T(1,128)} %bitcast.12, s32[1,32]{1,0:T(1,128)} %bitcast.13, s32[1,1]{1,0:T(1,128)} %bitcast.8.args_3_, s32[128,128]{1,0:T(8,128)} %bitcast.10, f32[128,128]{1,0:T(8,128)} %bitcast.11), custom_call_target="tpu_custom_call" | custom-call | tf_op jit(solution)/shard_map/pallas_call | solution.py:595
  25.9 0.6 %shard_map.78 = (f32[128,128]{1,0:T(8,128)}, f32[1,3]{1,0:T(1,128)}) custom-call(f32[128,128]{1,0:T(8,128)S(1)} %get-tuple-element.6.ranks_in, f32[1,128]{1,0:T(1,128)S(1)} %get-tuple-element.7.resid_in), custom_call_target="tpu_custom_call" | custom-call | tf_op jit(solution)/shard_map/pallas_call | solution.py:613
